TPU v7x, 32 devices: a whole 2x2x4 slice. The times are simulated.
32 devices in a mesh: mem: 8 (over z, x), grid: 4 (over y, core).
Axes of the slice: x: 2, y: 2, z: 4, core: 2. Of those that a mesh axis runs over, the one named last changes fastest.
Arguments:
- alpha: bfloat16 [16, 8, 768, 1536], P('mem', None, 'grid'), may hold values from -6 to 6
- perturbation: bfloat16 [16, 8, 768, 1536], P('mem', None, 'grid'), may hold values from -6 to 6
- legendre: bfloat16 [192, 128, 768], P('grid'), may hold values from -0.21875 to 0.21875
- response: float32 [192, 128], P('grid'), may hold values from 0.2 to 2
Outputs:
- increment: float32 [8, 768, 1536], P('mem', 'grid')
All inputs are finite; a program needn't handle non-finite values.
Results may differ from a plain program's by a relative error of at most 0.0063.
Values may be sent and summed in bfloat16 or wider, within the bound.
A program may use at most 128 MiB of HBM per device.

v0:
```python
import math
import jax
import jax.numpy as jnp
from jax import lax
from jax.sharding import PartitionSpec as P


def build_tables(lon_count, keep_dev, grid_count):
    col = jnp.arange(2 * keep_dev * grid_count, dtype=jnp.int32)
    block = col // (2 * keep_dev)
    part = col // keep_dev % 2
    wave = block * keep_dev + col % keep_dev
    lon = jnp.arange(lon_count, dtype=jnp.int32)
    phase = lon[:, None] * wave[None, :] % lon_count
    angle = phase.astype(jnp.float32) * jnp.float32(2.0 * math.pi / lon_count)
    basis = jnp.where(part[None, :] == 0, jnp.cos(angle), jnp.sin(angle))
    weight = jnp.where(wave == 0, jnp.float32(1.0), jnp.float32(2.0)) / jnp.float32(lon_count)
    forward = basis.astype(jnp.bfloat16)
    inverse = jnp.transpose(basis * weight[None, :]).astype(jnp.bfloat16)
    return (forward, inverse)


def legendre_filter(piece, legendre, response):
    cols, mem_dev, items, lat_count = piece.shape
    keep_dev = legendre.shape[0]
    split = piece.reshape(2, keep_dev, mem_dev, items, lat_count)
    coef = jnp.einsum("mnt,qmkit->qmkin", legendre, split, preferred_element_type=jnp.float32)
    coef = (coef * response[None, :, None, None, :]).astype(jnp.bfloat16)
    synth = jnp.einsum("mnt,qmkin->qmkit", legendre, coef, preferred_element_type=jnp.float32)
    return synth.astype(jnp.bfloat16).reshape(cols, mem_dev, items, lat_count)


def body(alpha, perturbation, legendre, response):
    mem_dev, levels, lat_dev, lon_count = alpha.shape
    keep_dev = legendre.shape[0]
    grid_count = lax.axis_size("grid")
    mem_count = lax.axis_size("mem")
    members = mem_dev * mem_count
    forward, inverse = build_tables(lon_count, keep_dev, grid_count)
    spectra = jnp.einsum("xc,klyx->ckly", forward, alpha, preferred_element_type=jnp.float32)
    spectra = spectra.astype(jnp.bfloat16)
    filtered = legendre_filter(
        lax.all_to_all(spectra, "grid", split_axis=0, concat_axis=3, tiled=True), legendre, response
    )
    returned = lax.all_to_all(filtered, "grid", split_axis=3, concat_axis=0, tiled=True)
    values = jnp.einsum("ckly,cx->klyx", returned, inverse, preferred_element_type=jnp.float32)
    total = lax.psum_scatter(
        jnp.sum(values * perturbation, axis=0), "mem", scatter_dimension=0, tiled=True
    )
    return total / jnp.sqrt(jnp.float32(members - 1))


def solution(mesh):
    placed = (
        P("mem", None, "grid", None),
        P("mem", None, "grid", None),
        P("grid", None, None),
        P("grid", None),
    )
    return jax.shard_map(
        body, mesh=mesh, in_specs=placed, out_specs=P("mem", "grid", None), check_vma=False
    )
```

profile of v0, /device:TPU:0, one launch (start us, length us, event | category | flops | bytes accessed | tf_op | source)
XLA Modules:
  0.0 337.0 jit_solution(17224794517558854112)
XLA Ops:
  6.6 17.5 %convolution_convert_fusion = bf16[384,2,8,192]{0,3,2,1:T(8,128)(2,1)} fusion(bf16[2,8,192,1536]{3,2,1,0:T(8,128)(2,1)} %param.4, s32[384]{0:T(512)S(1)} %fusion.57, pred[384]{0:T(512)(128)(4,1)S(1)} %fusion.59), kind=kOutput, calls=%fused_computation.25 | convolution fusion | flops 3631546368 | bytes 11798400 | tf_op jit(solution)/shard_map/xc,klyx->ckly/dot_general | solution.py:40
  24.1 4.0 %copy.15 = bf16[384,2,8,192]{3,2,1,0:T(8,128)(2,1)S(1)} copy(bf16[384,2,8,192]{0,3,2,1:T(8,128)(2,1)} %convolution_convert_fusion) | data formatting | bytes 4718592 | tf_op jit(solution)/shard_map/convert_element_type | solution.py:41
  28.1 41.0 %all_to_all.33 = bf16[384,2,8,192]{3,2,1,0:T(8,128)(2,1)S(1)} all-to-all(bf16[384,2,8,192]{3,2,1,0:T(8,128)(2,1)S(1)} %copy.15), channel_id=1, replica_groups=mesh['mem'=8,'grid'=4] {'grid'}, dimensions={0} | all-to-all | bytes 4718592 | tf_op jit(solution)/shard_map/all_to_all | solution.py:43
  69.1 4.0 %copy.40 = bf16[4,96,2,8,192]{4,0,3,2,1:T(4,128)(2,1)S(1)} copy(bf16[4,96,2,8,192]{4,3,2,1,0:T(8,128)(2,1)S(1)} %bitcast.48) | data formatting | bytes 4718592 | tf_op jit(solution)/shard_map/all_to_all | solution.py:43
  73.1 0.0 copy-start
  73.1 3.8 %reshape.57 = bf16[2,48,2,8,768]{4,3,2,1,0:T(8,128)(2,1)} reshape(bf16[96,2,8,4,192]{4,3,2,1,0:T(4,128)(2,1)S(1)} %bitcast.49) | data formatting | bytes 4718592 | tf_op jit(solution)/shard_map/reshape | solution.py:26
  76.9 0.0 copy-done
  76.9 11.5 %convert_bitcast_fusion = bf16[2,48,2,8,768]{4,3,2,0,1:T(8,128)(2,1)S(1)} fusion(bf16[48,128,768]{2,1,0:T(8,128)(2,1)} %param.6, bf16[2,48,2,8,768]{4,3,2,1,0:T(8,128)(2,1)} %reshape.57, f32[48,128]{1,0:T(8,128)S(1)} %copy-done), kind=kOutput, calls=%fused_computation.18 | convolution fusion | flops 605552640 | bytes 14180352 | tf_op jit(solution)/shard_map/mnt,qmkin->qmkit/dot_general | solution.py:29
  88.4 1.6 copy.18
  90.1 5.3 %copy.19 = bf16[96,2,8,768]{0,2,1,3:T(8,128)(2,1)} copy(bf16[96,2,8,768]{3,2,1,0:T(8,128)(2,1)} %bitcast.51) | data formatting | bytes 4718592 | tf_op jit(solution)/shard_map/reshape | solution.py:30
  95.4 3.7 %all-to-all-start.1 = ((bf16[96,2,8,768]{0,2,1,3:T(8,128)(2,1)}), bf16[96,2,8,768]{0,2,1,3:T(8,128)(2,1)S(1)}, u32[]{:S(2)}, u32[]{:S(2)}) async-start(bf16[96,2,8,768]{0,2,1,3:T(8,128)(2,1)} %copy.19), calls=%async_computation.1 | async-start | bytes 6291456 | tf_op jit(solution)/shard_map/all_to_all | solution.py:45
  99.1 0.3 reduce-scatter.2.cloned.1.call-start
  99.4 36.6 %all-to-all-done.1 = bf16[96,2,8,768]{0,2,1,3:T(8,128)(2,1)S(1)} async-done(((bf16[96,2,8,768]{0,2,1,3:T(8,128)(2,1)}), bf16[96,2,8,768]{0,2,1,3:T(8,128)(2,1)S(1)}, u32[]{:S(2)}, u32[]{:S(2)}) %all-to-all-start.1) | async-done | bytes 2359328 | tf_op jit(solution)/shard_map/all_to_all | solution.py:45
  135.9 4.1 %copy.39 = bf16[96,2,8,4,192]{0,3,4,2,1:T(4,128)(2,1)} copy(bf16[96,2,8,4,192]{0,2,1,4,3:T(8,128)(2,1)S(1)} %bitcast.47) | data formatting | bytes 4718592 | tf_op jit(solution)/shard_map/all_to_all | solution.py:45
  140.0 5.0 %all_to_all.30 = bf16[384,2,8,192]{0,3,2,1:T(8,128)(2,1)S(1)} reshape(bf16[4,96,2,8,192]{1,0,4,3,2:T(4,128)(2,1)} %bitcast.50) | data formatting | bytes 4718592 | tf_op jit(solution)/shard_map/all_to_all | solution.py:45
  145.0 20.1 %multiply_reduce_fusion = f32[8,192,1536]{2,1,0:T(8,128)} fusion(bf16[2,8,192,1536]{3,2,1,0:T(8,128)(2,1)} %param.5, bf16[384,2,8,192]{0,3,2,1:T(8,128)(2,1)S(1)} %all_to_all.30, f32[384]{0:T(512)S(1)} %select_multiply_fusion, s32[384]{0:T(512)S(1)} %fusion.57, pred[384]{0:T(512)(128)(4,1)S(1)} %fusion.59), kind=kOutput, calls=%fused_computation | convolution fusion | flops 3642753024 | bytes 21237120 | tf_op jit(solution)/shard_map/ckly,cx->klyx/dot_general | solution.py:46
  165.1 0.0 reduce-scatter.2.cloned.1.call-update
  165.2 162.6 %reduce-scatter.2.cloned.1.call-done = f32[1,192,1536]{2,1,0:T(8,128)} async-done(((f32[8,192,1536]{2,1,0:T(8,128)}), f32[1,192,1536]{2,1,0:T(8,128)}) %reduce-scatter.2.cloned.1.call-update) | async-done | bytes 1179664 | tf_op jit(solution)/shard_map/reduce_scatter | solution.py:47
  327.7 2.4 broadcast_multiply_fusion
  (3 shorter events, 0.0 us)
Async XLA Ops:
  73.1 3.8 %copy-start = (f32[48,128]{1,0:T(8,128)S(1)}, f32[48,128]{1,0:T(8,128)}, u32[]{:S(2)}) copy-start(f32[48,128]{1,0:T(8,128)} %param.7) | copy-start | bytes 73732
  95.4 40.6 %all-to-all-start.1 = ((bf16[96,2,8,768]{0,2,1,3:T(8,128)(2,1)}), bf16[96,2,8,768]{0,2,1,3:T(8,128)(2,1)S(1)}, u32[]{:S(2)}, u32[]{:S(2)}) async-start(bf16[96,2,8,768]{0,2,1,3:T(8,128)(2,1)} %copy.19), calls=%async_computation.1 | async-start | bytes 6291456 | tf_op jit(solution)/shard_map/all_to_all | solution.py:45
  99.1 228.7 %reduce-scatter.2.cloned.1.call-start = ((), (), s32[]{:S(2)}) async-start(), calls=%async_computation.3 | async-start | bytes 10616832 | tf_op jit(solution)/shard_map/reduce_scatter | solution.py:47
Sparse Core Ops, SparseCore 0:
  165.3 162.3 reduce-scatter.1
where the time goes:
time: 337 us
  waiting for transfers between devices  199 us (59%)
  matrix products  49.2 us (15%)
  blocking collectives  41 us (12%)
  local copies, waits for them, and re-layouts  27.8 us (8%)
  between operations  13.5 us (4%)
  starting transfers between devices  3.96 us (1%)
    reduce_scatter x1, waiting for transfers between devices, body(): lax.psum_scatter(jnp.sum(values * perturbation, axis=0), 'mem', scatter_d...  163 us
    all_to_all x1, blocking collectives, body(): lax.all_to_all(spectra, 'grid', split_axis=0, concat_axis=3, tiled=True)  41 us
    all_to_all x1, waiting for transfers between devices, body(): lax.all_to_all(filtered, 'grid', split_axis=3, concat_axis=0, tiled=True)  36.6 us
    dot_general x1, matrix products, body(): jnp.einsum('ckly,cx->klyx', returned, inverse, preferred_element_type=jnp...  20.1 us
    dot_general x1, matrix products, body(): jnp.einsum('xc,klyx->ckly', forward, alpha, preferred_element_type=jnp.fl...  17.5 us
    dot_general x1, matrix products, legendre_filter(): jnp.einsum('mnt,qmkin->qmkit', legendre, coef, preferred_element_type=jnp...  11.5 us
    all_to_all x2, local copies, waits for them, and re-layouts, body(): lax.all_to_all(filtered, 'grid', split_axis=3, concat_axis=0, tiled=True)  9.05 us
  transfers between devices with their start and end apart: 2, of which 2 were waited for; matrix products, arithmetic and copies ran while one was open for 0% of the time, Pallas kernels for 0%

commit v1 on v0

--- a/solution.py
+++ b/solution.py
@@ -3,6 +3,28 @@
 import jax.numpy as jnp
 from jax import lax
 from jax.sharding import PartitionSpec as P
+
+
+def in_blocks(array, dim, devices):
+    before, after = (array.shape[:dim], array.shape[dim + 1 :])
+    return jnp.moveaxis(array.reshape(*before, devices, -1, *after), dim, 0)
+
+
+def in_order(tiles, dim):
+    tiles = jnp.moveaxis(tiles, 0, dim)
+    dims = tiles.shape
+    return tiles.reshape(*dims[:dim], dims[dim] * dims[dim + 1], *dims[dim + 2 :])
+
+
+def rotated_exchange(shard, axis, split_dim, concat_dim):
+    size, index = (lax.axis_size(axis), lax.axis_index(axis))
+    pieces = in_blocks(shard, split_dim, size)
+    done = [pieces[index]]
+    for turn in range(1, size):
+        sent = pieces[(index + turn) % size]
+        done.append(lax.ppermute(sent, axis, [(i, (i + turn) % size) for i in range(size)]))
+    pieces = jnp.stack(done)[(index - jnp.arange(size)) % size]
+    return in_order(pieces, concat_dim)
 
 
 def build_tables(lon_count, keep_dev, grid_count):
@@ -39,9 +61,7 @@
     forward, inverse = build_tables(lon_count, keep_dev, grid_count)
     spectra = jnp.einsum("xc,klyx->ckly", forward, alpha, preferred_element_type=jnp.float32)
     spectra = spectra.astype(jnp.bfloat16)
-    filtered = legendre_filter(
-        lax.all_to_all(spectra, "grid", split_axis=0, concat_axis=3, tiled=True), legendre, response
-    )
+    filtered = legendre_filter(rotated_exchange(spectra, "grid", 0, 3), legendre, response)
     returned = lax.all_to_all(filtered, "grid", split_axis=3, concat_axis=0, tiled=True)
     values = jnp.einsum("ckly,cx->klyx", returned, inverse, preferred_element_type=jnp.float32)
     total = lax.psum_scatter(

time: 337 us -> 340 us (level)
  blocking collectives: 41 us -> 0 us
  waiting for transfers between devices: 199 us -> 234 us
  local copies, waits for them, and re-layouts: 27.8 us -> 32.3 us
    all_to_all x1 -> x0, blocking collectives: 41 us -> none  [body(): lax.all_to_all(spectra, 'grid', split_axis=0, concat_axis=3, tiled=True)]
    ppermute x0 -> x3, waiting for transfers between devices: none -> 34.8 us  [rotated_exchange(): lax.ppermute(sent, axis, [(i, (i + turn) % size) for i in range(size)])]
    transpose x0 -> x1, local copies, waits for them, and re-layouts: none -> 5.94 us  [in_order(): tiles = jnp.moveaxis(tiles, 0, dim)]
    all_to_all x1 -> x0, local copies, waits for them, and re-layouts: 4.05 us -> none  [body(): lax.all_to_all(spectra, 'grid', split_axis=0, concat_axis=3, tiled=True)]
    convert_element_type x1 -> x0, local copies, waits for them, and re-layouts: 4.03 us -> none  [body(): spectra = spectra.astype(jnp.bfloat16)]
    another operation x0 -> x1, local copies, waits for them, and re-layouts: none -> 3.8 us  [legendre_filter(): split = piece.reshape(2, keep_dev, mem_dev, items, lat_count)]
  transfers between devices with their start and end apart: 2 -> 5, of which waited for: 2 -> 4; matrix products, arithmetic and copies ran while one was open for 0% -> 0% of each run, Pallas kernels for 0% -> 0%
where the time goes in v1:
time: 340 us
  waiting for transfers between devices  234 us (69%)
  matrix products  49.2 us (14%)
  local copies, waits for them, and re-layouts  32.3 us (9%)
  between operations  13.5 us (4%)
  starting transfers between devices  7.23 us (2%)
    reduce_scatter x1, waiting for transfers between devices, body(): lax.psum_scatter(jnp.sum(values * perturbation, axis=0), 'mem', scatter_d...  163 us
    all_to_all x1, waiting for transfers between devices, body(): lax.all_to_all(filtered, 'grid', split_axis=3, concat_axis=0, tiled=True)  36.6 us
    ppermute x3, waiting for transfers between devices, rotated_exchange(): lax.ppermute(sent, axis, [(i, (i + turn) % size) for i in range(size)])  34.8 us
    dot_general x1, matrix products, body(): jnp.einsum('ckly,cx->klyx', returned, inverse, preferred_element_type=jnp...  20.1 us
    dot_general x1, matrix products, body(): jnp.einsum('xc,klyx->ckly', forward, alpha, preferred_element_type=jnp.fl...  17.5 us
    dot_general x1, matrix products, legendre_filter(): jnp.einsum('mnt,qmkin->qmkit', legendre, coef, preferred_element_type=jnp...  11.6 us
    all_to_all x2, local copies, waits for them, and re-layouts, body(): lax.all_to_all(filtered, 'grid', split_axis=3, concat_axis=0, tiled=True)  9.03 us
  transfers between devices with their start and end apart: 5, of which 4 were waited for; matrix products, arithmetic and copies ran while one was open for 0% of the time, Pallas kernels for 0%

profile of v1, /device:TPU:0, one launch (start us, length us, event | category | flops | bytes accessed | tf_op | source)
XLA Modules:
  0.0 339.7 jit_solution(325998615780174811)
XLA Ops:
  6.6 17.5 %convolution_convert_fusion = bf16[384,2,8,192]{0,3,2,1:T(8,128)(2,1)} fusion(bf16[2,8,192,1536]{3,2,1,0:T(8,128)(2,1)} %param.4, s32[384]{0:T(512)S(1)} %fusion.57, pred[384]{0:T(512)(128)(4,1)S(1)} %fusion.59), kind=kOutput, calls=%fused_computation.26 | convolution fusion | flops 3631546368 | bytes 11798400 | tf_op jit(solution)/shard_map/xc,klyx->ckly/dot_general | solution.py:62
  24.1 4.0 %copy.37 = bf16[384,2,8,192]{3,2,1,0:T(8,128)(2,1)S(1)} copy(bf16[384,2,8,192]{0,3,2,1:T(8,128)(2,1)} %convolution_convert_fusion) | data formatting | bytes 4718592 | tf_op jit(solution)/shard_map/reshape | solution.py:10
  28.1 0.2 constant_dynamic-slice_fusion
  28.3 2.5 collective-permute-start.2
  30.8 0.6 collective-permute-start.1
  31.5 0.2 collective-permute-start
  31.6 17.0 %collective-permute-done.2 = bf16[96,2,8,192]{3,2,1,0:T(8,128)(2,1)S(1)} collective-permute-done((bf16[96,2,8,192]{3,2,1,0:T(8,128)(2,1)S(1)}, bf16[96,2,8,192]{3,2,1,0:T(8,128)(2,1)S(1)}, u32[]{:S(2)}, u32[]{:S(2)}) %collective-permute-start.2) | collective-permute-done | bytes 589856 | tf_op jit(solution)/shard_map/ppermute | solution.py:25
  48.7 17.8 %collective-permute-done.1 = bf16[96,2,8,192]{3,2,1,0:T(8,128)(2,1)S(1)} collective-permute-done((bf16[96,2,8,192]{3,2,1,0:T(8,128)(2,1)S(1)}, bf16[96,2,8,192]{3,2,1,0:T(8,128)(2,1)S(1)}, u32[]{:S(2)}, u32[]{:S(2)}) %collective-permute-start.1) | collective-permute-done | bytes 589856 | tf_op jit(solution)/shard_map/ppermute | solution.py:25
  66.5 0.8 pad_maximum_fusion
  67.3 2.4 gather_fusion
  69.7 5.9 %copy.26 = bf16[96,2,8,4,192]{4,3,2,1,0:T(4,128)(2,1)S(1)} copy(bf16[96,2,8,4,192]{4,2,1,0,3:T(8,128)(2,1)} %bitcast.57) | data formatting | bytes 4718592 | tf_op jit(solution)/shard_map/transpose | solution.py:14
  75.6 3.8 %reshape_reshape.3 = bf16[2,48,2,8,768]{4,3,2,1,0:T(8,128)(2,1)} reshape(bf16[96,2,8,4,192]{4,3,2,1,0:T(4,128)(2,1)S(1)} %copy.26) | data formatting | bytes 4718592 | tf_op jit(solution)/shard_map/reshape;reshape | solution.py:48
  79.4 11.6 %convert_bitcast_fusion = bf16[2,48,2,8,768]{4,3,2,0,1:T(8,128)(2,1)S(1)} fusion(bf16[48,128,768]{2,1,0:T(8,128)(2,1)} %param.6, bf16[2,48,2,8,768]{4,3,2,1,0:T(8,128)(2,1)} %reshape_reshape.3, f32[48,128]{1,0:T(8,128)S(1)} %copy-done), kind=kOutput, calls=%fused_computation.19 | convolution fusion | flops 605552640 | bytes 14180352 | tf_op jit(solution)/shard_map/mnt,qmkin->qmkit/dot_general | solution.py:51
  91.1 1.6 copy.28
  92.7 5.3 %copy.29 = bf16[96,2,8,768]{0,2,1,3:T(8,128)(2,1)} copy(bf16[96,2,8,768]{3,2,1,0:T(8,128)(2,1)} %bitcast.60) | data formatting | bytes 4718592 | tf_op jit(solution)/shard_map/reshape | solution.py:52
  98.0 3.7 %all-to-all-start = ((bf16[96,2,8,768]{0,2,1,3:T(8,128)(2,1)}), bf16[96,2,8,768]{0,2,1,3:T(8,128)(2,1)S(1)}, u32[]{:S(2)}, u32[]{:S(2)}) async-start(bf16[96,2,8,768]{0,2,1,3:T(8,128)(2,1)} %copy.29), calls=%async_computation | async-start | bytes 6291456 | tf_op jit(solution)/shard_map/all_to_all | solution.py:65
  101.7 0.3 reduce-scatter.2.cloned.1.call-start
  102.0 36.6 %all-to-all-done = bf16[96,2,8,768]{0,2,1,3:T(8,128)(2,1)S(1)} async-done(((bf16[96,2,8,768]{0,2,1,3:T(8,128)(2,1)}), bf16[96,2,8,768]{0,2,1,3:T(8,128)(2,1)S(1)}, u32[]{:S(2)}, u32[]{:S(2)}) %all-to-all-start) | async-done | bytes 2359328 | tf_op jit(solution)/shard_map/all_to_all | solution.py:65
  138.6 4.1 %copy.49 = bf16[96,2,8,4,192]{0,3,4,2,1:T(4,128)(2,1)} copy(bf16[96,2,8,4,192]{0,2,1,4,3:T(8,128)(2,1)S(1)} %bitcast.56) | data formatting | bytes 4718592 | tf_op jit(solution)/shard_map/all_to_all | solution.py:65
  142.6 5.0 %all_to_all.16 = bf16[384,2,8,192]{0,3,2,1:T(8,128)(2,1)S(1)} reshape(bf16[4,96,2,8,192]{1,0,4,3,2:T(4,128)(2,1)} %bitcast.59) | data formatting | bytes 4718592 | tf_op jit(solution)/shard_map/all_to_all | solution.py:65
  147.6 20.1 %multiply_reduce_fusion = f32[8,192,1536]{2,1,0:T(8,128)} fusion(bf16[2,8,192,1536]{3,2,1,0:T(8,128)(2,1)} %param.5, bf16[384,2,8,192]{0,3,2,1:T(8,128)(2,1)S(1)} %all_to_all.16, f32[384]{0:T(512)S(1)} %select_multiply_fusion, s32[384]{0:T(512)S(1)} %fusion.57, pred[384]{0:T(512)(128)(4,1)S(1)} %fusion.59), kind=kOutput, calls=%fused_computation.1 | convolution fusion | flops 3642753024 | bytes 21237120 | tf_op jit(solution)/shard_map/ckly,cx->klyx/dot_general | solution.py:66
  167.7 0.0 reduce-scatter.2.cloned.1.call-update
  167.8 162.7 %reduce-scatter.2.cloned.1.call-done = f32[1,192,1536]{2,1,0:T(8,128)} async-done(((f32[8,192,1536]{2,1,0:T(8,128)}), f32[1,192,1536]{2,1,0:T(8,128)}) %reduce-scatter.2.cloned.1.call-update) | async-done | bytes 1179664 | tf_op jit(solution)/shard_map/reduce_scatter | solution.py:67
  330.5 2.4 broadcast_multiply_fusion
  (8 shorter events, 0.1 us)
Async XLA Ops:
  28.3 20.3 %collective-permute-start.2 = (bf16[96,2,8,192]{3,2,1,0:T(8,128)(2,1)S(1)}, bf16[96,2,8,192]{3,2,1,0:T(8,128)(2,1)S(1)}, u32[]{:S(2)}, u32[]{:S(2)}) collective-permute-start(bf16[96,2,8,192]{3,2,1,0:T(8,128)(2,1)S(1)} %get-tuple-element.6), channel_id=1, source_target_pairs={{0,3},{1,0},{2,1},{3,2},{4,7},{5,4},{6,5},{7,6},{8,11},{9,8},{10,9... | collective-permute-start | bytes 1769480 | tf_op jit(solution)/shard_map/ppermute | solution.py:25
  30.8 35.6 %collective-permute-start.1 = (bf16[96,2,8,192]{3,2,1,0:T(8,128)(2,1)S(1)}, bf16[96,2,8,192]{3,2,1,0:T(8,128)(2,1)S(1)}, u32[]{:S(2)}, u32[]{:S(2)}) collective-permute-start(bf16[96,2,8,192]{3,2,1,0:T(8,128)(2,1)S(1)} %get-tuple-element.7), channel_id=1, source_target_pairs={{0,2},{1,3},{2,0},{3,1},{4,6},{5,7},{6,4},{7,5},{8,10},{9,11},{10,... | collective-permute-start | bytes 1769480 | tf_op jit(solution)/shard_map/ppermute | solution.py:25
  31.5 35.0 %collective-permute-start = (bf16[96,2,8,192]{3,2,1,0:T(8,128)(2,1)S(1)}, bf16[96,2,8,192]{3,2,1,0:T(8,128)(2,1)S(1)}, u32[]{:S(2)}, u32[]{:S(2)}) collective-permute-start(bf16[96,2,8,192]{3,2,1,0:T(8,128)(2,1)S(1)} %get-tuple-element.8), channel_id=1, source_target_pairs={{0,1},{1,2},{2,3},{3,0},{4,5},{5,6},{6,7},{7,4},{8,9},{9,10},{10,1... | collective-permute-start | bytes 1769480 | tf_op jit(solution)/shard_map/ppermute | solution.py:25
  75.6 3.8 %copy-start = (f32[48,128]{1,0:T(8,128)S(1)}, f32[48,128]{1,0:T(8,128)}, u32[]{:S(2)}) copy-start(f32[48,128]{1,0:T(8,128)} %param.7) | copy-start | bytes 73732
  98.0 40.6 %all-to-all-start = ((bf16[96,2,8,768]{0,2,1,3:T(8,128)(2,1)}), bf16[96,2,8,768]{0,2,1,3:T(8,128)(2,1)S(1)}, u32[]{:S(2)}, u32[]{:S(2)}) async-start(bf16[96,2,8,768]{0,2,1,3:T(8,128)(2,1)} %copy.29), calls=%async_computation | async-start | bytes 6291456 | tf_op jit(solution)/shard_map/all_to_all | solution.py:65
  101.7 228.8 %reduce-scatter.2.cloned.1.call-start = ((), (), s32[]{:S(2)}) async-start(), calls=%async_computation.2 | async-start | bytes 10616832 | tf_op jit(solution)/shard_map/reduce_scatter | solution.py:67
Sparse Core Ops, SparseCore 0:
  167.9 162.5 reduce-scatter.1
